TPU v7x, 32 devices: a whole 2x2x4 slice. The times are simulated.
32 devices in a mesh: scen: 2 (over y), cell: 4 (over z), obs: 4 (over x, core).
Axes of the slice: x: 2, y: 2, z: 4, core: 2. Of those that a mesh axis runs over, the one named last changes fastest.
Arguments:
- prior: bfloat16 [400, 2048], P('scen', 'cell'), parts along dimension 0, may hold values from -6 to 6
- obs_block: int32 [4096], P('obs'), may hold values from 0 to 15
- obs_weight: bfloat16 [4096, 128], P('obs'), may hold values from -0.5 to 0.5
- observed: float32 [8192], P(('scen', 'obs')), parts along dimension 0, may hold values from -8 to 8
- obs_sigma: float32 [4096], P('obs'), may hold values from 0.5 to 1.5
- pert_seed: int32 [6, 200, 4096], P('scen', None, 'obs'), parts along dimension 0, may hold values from 0 to 1048575
Outputs:
- posterior: bfloat16 [400, 2048], P('scen', 'cell'), parts along dimension 0
- post_predicted: float32 [400, 4096], P('scen', 'obs'), parts along dimension 0
There are 2 independent parts, one for each index of `scen`. A program takes and returns all parts, laid end to end along the dimension named above; an argument that names none is the same for every part. Nothing has to cross between parts.
All inputs are finite; a program needn't handle non-finite values.
Results may differ from a plain program's by a relative error of at most 0.0013.
Values sent between devices are 32-bit elements; how exact they have to be, the bound alone decides.
A program may use at most 64 MiB of HBM per device.

v0:
```python
import jax
import jax.numpy as jnp
from jax import lax
from jax.sharding import PartitionSpec as P

BLK = 128
ITERS = 3


def local_partial(param_field, local_index, weights):
    members = param_field.shape[0]
    nblocks = param_field.shape[1] // BLK
    blocks = param_field.reshape(members, nblocks, BLK)
    obs_count = local_index.shape[0]
    groups = obs_count // 64
    indices = local_index.reshape(groups, 64)
    group_weights = weights.reshape(groups, 64, BLK)

    def one_group(operands):
        group_index, group_weight = operands
        picked = jnp.take(blocks, group_index, axis=1)
        return jnp.sum(picked * group_weight[None], axis=2)

    result = lax.map(one_group, (indices, group_weights))
    return jnp.transpose(result, (1, 0, 2)).reshape(members, obs_count)


def per_device(prior, obs_block, obs_weight, observed, obs_sigma, pert_seed):
    members = prior.shape[0]
    nblocks = prior.shape[1] // BLK
    hp = lax.Precision.HIGHEST
    first_block = lax.axis_index("cell") * nblocks
    local_block = obs_block - first_block
    inside = jnp.logical_and(local_block >= 0, local_block < nblocks)
    clipped = jnp.clip(local_block, 0, nblocks - 1)
    weights = obs_weight.astype(jnp.float32) * inside[:, None].astype(jnp.float32)
    param_field = prior.astype(jnp.float32)
    inflation = jnp.float32(ITERS)
    root_scale = jnp.sqrt(jnp.float32(members - 1.0))
    identity = jnp.eye(members, dtype=jnp.float32)
    partial_terms = local_partial(param_field, clipped, weights)
    predicted = lax.psum(partial_terms, "cell")
    for step_index in range(ITERS):
        noise = jnp.sqrt(jnp.float32(3.0)) * (
            (2.0 * pert_seed[step_index].astype(jnp.float32) + 1.0) / 1048576.0 - 1.0
        )
        misfit = observed[None, :] + jnp.sqrt(inflation) * obs_sigma[None, :] * noise - predicted
        dev_pred = predicted - jnp.mean(predicted, axis=0, keepdims=True)
        dev_field = param_field - jnp.mean(param_field, axis=0, keepdims=True)
        scaled_dev = dev_pred / (obs_sigma[None, :] * root_scale)
        scaled_misfit = misfit / obs_sigma[None, :]
        gram_matrix = jnp.dot(scaled_dev, scaled_dev.T, precision=hp)
        cross_term = jnp.dot(scaled_dev, scaled_misfit.T, precision=hp)
        gram_matrix, cross_term = lax.psum((gram_matrix, cross_term), "obs")
        factor = jnp.linalg.cholesky(gram_matrix + inflation * identity)
        member_weight = jax.scipy.linalg.cho_solve((factor, True), cross_term)
        param_field = param_field + jnp.dot(member_weight.T, dev_field, precision=hp) / root_scale
        predicted = predicted + jnp.dot(member_weight.T, dev_pred, precision=hp) / root_scale
    return (param_field.astype(jnp.bfloat16), predicted)


def solution(mesh):
    return jax.shard_map(
        per_device,
        mesh=mesh,
        in_specs=(
            P("scen", "cell"),
            P("obs"),
            P("obs", None),
            P(("scen", "obs")),
            P("obs"),
            P("scen", None, "obs"),
        ),
        out_specs=(P("scen", "cell"), P("scen", "obs")),
        check_vma=False,
    )
```

profile of v0, /device:TPU:0, one launch (start us, length us, event | category | flops | bytes accessed | tf_op | source)
XLA Modules:
  0.0 502.5 jit_solution(17134970231463933520)
XLA Ops:
  10.8 143.9 %while.14 = (s32[]{:T(128)}, f32[16,200,64]{1,2,0:T(8,128)S(1)}, s32[16,64]{1,0:T(8,128)S(1)}, f32[200,4,128]{2,0,1:T(8,128)S(1)}, f32[16,64,128]{2,1,0:T(8,128)S(1)}, /*index=5*/s32[]{:T(128)}) while((s32[]{:T(128)}, f32[16,200,64]{1,2,0:T(8,128)S(1)}, s32[16,64]{1,0:T(8,128)S(1)}, f32[200,4,128]{2,0,1:T(8,128)S(1)}, ...), condition=%wide.region_2.3_spmd, body=%wide.region_0.2_spmd.sunk | while | flops 4904002 | bytes 19946964 | solution.py:24
  10.9 3.7 gather_fusion
  14.6 5.2 %multiply_reduce_fusion.2 = f32[64,200]{1,0:T(8,128)S(1)} fusion(f32[64,200,128]{2,1,0:T(8,128)} %gather_fusion, f32[64,128]{1,0:T(8,128)S(1)} %dynamic-slice_bitcast_fusion.2, pred[64]{0:T(512)(128)(4,1)S(1)} %compare_and_fusion.2), kind=kLoop, calls=%fused_computation.1.clone.1 | loop fusion | flops 4902400 | bytes 6637632 | tf_op jit(solution)/shard_map/while/body/eval_jaxpr/reduce_sum | solution.py:22
  19.8 3.7 gather_fusion
  23.6 5.2 %multiply_reduce_fusion.2 = f32[64,200]{1,0:T(8,128)S(1)} fusion(f32[64,200,128]{2,1,0:T(8,128)} %gather_fusion, f32[64,128]{1,0:T(8,128)S(1)} %dynamic-slice_bitcast_fusion.2, pred[64]{0:T(512)(128)(4,1)S(1)} %compare_and_fusion.2), kind=kLoop, calls=%fused_computation.1.clone.1 | loop fusion | flops 4902400 | bytes 6637632 | tf_op jit(solution)/shard_map/while/body/eval_jaxpr/reduce_sum | solution.py:22
  28.8 3.7 gather_fusion
  32.6 5.2 %multiply_reduce_fusion.2 = f32[64,200]{1,0:T(8,128)S(1)} fusion(f32[64,200,128]{2,1,0:T(8,128)} %gather_fusion, f32[64,128]{1,0:T(8,128)S(1)} %dynamic-slice_bitcast_fusion.2, pred[64]{0:T(512)(128)(4,1)S(1)} %compare_and_fusion.2), kind=kLoop, calls=%fused_computation.1.clone.1 | loop fusion | flops 4902400 | bytes 6637632 | tf_op jit(solution)/shard_map/while/body/eval_jaxpr/reduce_sum | solution.py:22
  37.8 3.7 gather_fusion
  41.6 5.2 %multiply_reduce_fusion.2 = f32[64,200]{1,0:T(8,128)S(1)} fusion(f32[64,200,128]{2,1,0:T(8,128)} %gather_fusion, f32[64,128]{1,0:T(8,128)S(1)} %dynamic-slice_bitcast_fusion.2, pred[64]{0:T(512)(128)(4,1)S(1)} %compare_and_fusion.2), kind=kLoop, calls=%fused_computation.1.clone.1 | loop fusion | flops 4902400 | bytes 6637632 | tf_op jit(solution)/shard_map/while/body/eval_jaxpr/reduce_sum | solution.py:22
  46.8 3.7 gather_fusion
  50.6 5.2 %multiply_reduce_fusion.2 = f32[64,200]{1,0:T(8,128)S(1)} fusion(f32[64,200,128]{2,1,0:T(8,128)} %gather_fusion, f32[64,128]{1,0:T(8,128)S(1)} %dynamic-slice_bitcast_fusion.2, pred[64]{0:T(512)(128)(4,1)S(1)} %compare_and_fusion.2), kind=kLoop, calls=%fused_computation.1.clone.1 | loop fusion | flops 4902400 | bytes 6637632 | tf_op jit(solution)/shard_map/while/body/eval_jaxpr/reduce_sum | solution.py:22
  55.8 3.7 gather_fusion
  59.5 5.2 %multiply_reduce_fusion.2 = f32[64,200]{1,0:T(8,128)S(1)} fusion(f32[64,200,128]{2,1,0:T(8,128)} %gather_fusion, f32[64,128]{1,0:T(8,128)S(1)} %dynamic-slice_bitcast_fusion.2, pred[64]{0:T(512)(128)(4,1)S(1)} %compare_and_fusion.2), kind=kLoop, calls=%fused_computation.1.clone.1 | loop fusion | flops 4902400 | bytes 6637632 | tf_op jit(solution)/shard_map/while/body/eval_jaxpr/reduce_sum | solution.py:22
  64.8 3.7 gather_fusion
  68.5 5.2 %multiply_reduce_fusion.2 = f32[64,200]{1,0:T(8,128)S(1)} fusion(f32[64,200,128]{2,1,0:T(8,128)} %gather_fusion, f32[64,128]{1,0:T(8,128)S(1)} %dynamic-slice_bitcast_fusion.2, pred[64]{0:T(512)(128)(4,1)S(1)} %compare_and_fusion.2), kind=kLoop, calls=%fused_computation.1.clone.1 | loop fusion | flops 4902400 | bytes 6637632 | tf_op jit(solution)/shard_map/while/body/eval_jaxpr/reduce_sum | solution.py:22
  73.8 3.7 gather_fusion
  77.5 5.2 %multiply_reduce_fusion.2 = f32[64,200]{1,0:T(8,128)S(1)} fusion(f32[64,200,128]{2,1,0:T(8,128)} %gather_fusion, f32[64,128]{1,0:T(8,128)S(1)} %dynamic-slice_bitcast_fusion.2, pred[64]{0:T(512)(128)(4,1)S(1)} %compare_and_fusion.2), kind=kLoop, calls=%fused_computation.1.clone.1 | loop fusion | flops 4902400 | bytes 6637632 | tf_op jit(solution)/shard_map/while/body/eval_jaxpr/reduce_sum | solution.py:22
  82.8 3.7 gather_fusion
  86.5 5.2 %multiply_reduce_fusion.2 = f32[64,200]{1,0:T(8,128)S(1)} fusion(f32[64,200,128]{2,1,0:T(8,128)} %gather_fusion, f32[64,128]{1,0:T(8,128)S(1)} %dynamic-slice_bitcast_fusion.2, pred[64]{0:T(512)(128)(4,1)S(1)} %compare_and_fusion.2), kind=kLoop, calls=%fused_computation.1.clone.1 | loop fusion | flops 4902400 | bytes 6637632 | tf_op jit(solution)/shard_map/while/body/eval_jaxpr/reduce_sum | solution.py:22
  91.8 3.7 gather_fusion
  95.5 5.2 %multiply_reduce_fusion.2 = f32[64,200]{1,0:T(8,128)S(1)} fusion(f32[64,200,128]{2,1,0:T(8,128)} %gather_fusion, f32[64,128]{1,0:T(8,128)S(1)} %dynamic-slice_bitcast_fusion.2, pred[64]{0:T(512)(128)(4,1)S(1)} %compare_and_fusion.2), kind=kLoop, calls=%fused_computation.1.clone.1 | loop fusion | flops 4902400 | bytes 6637632 | tf_op jit(solution)/shard_map/while/body/eval_jaxpr/reduce_sum | solution.py:22
  100.8 3.7 gather_fusion
  104.5 5.2 %multiply_reduce_fusion.2 = f32[64,200]{1,0:T(8,128)S(1)} fusion(f32[64,200,128]{2,1,0:T(8,128)} %gather_fusion, f32[64,128]{1,0:T(8,128)S(1)} %dynamic-slice_bitcast_fusion.2, pred[64]{0:T(512)(128)(4,1)S(1)} %compare_and_fusion.2), kind=kLoop, calls=%fused_computation.1.clone.1 | loop fusion | flops 4902400 | bytes 6637632 | tf_op jit(solution)/shard_map/while/body/eval_jaxpr/reduce_sum | solution.py:22
  109.8 3.7 gather_fusion
  113.5 5.2 %multiply_reduce_fusion.2 = f32[64,200]{1,0:T(8,128)S(1)} fusion(f32[64,200,128]{2,1,0:T(8,128)} %gather_fusion, f32[64,128]{1,0:T(8,128)S(1)} %dynamic-slice_bitcast_fusion.2, pred[64]{0:T(512)(128)(4,1)S(1)} %compare_and_fusion.2), kind=kLoop, calls=%fused_computation.1.clone.1 | loop fusion | flops 4902400 | bytes 6637632 | tf_op jit(solution)/shard_map/while/body/eval_jaxpr/reduce_sum | solution.py:22
  122.5 5.2 %multiply_reduce_fusion.2 = f32[64,200]{1,0:T(8,128)S(1)} fusion(f32[64,200,128]{2,1,0:T(8,128)} %gather_fusion, f32[64,128]{1,0:T(8,128)S(1)} %dynamic-slice_bitcast_fusion.2, pred[64]{0:T(512)(128)(4,1)S(1)} %compare_and_fusion.2), kind=kLoop, calls=%fused_computation.1.clone.1 | loop fusion | flops 4902400 | bytes 6637632 | tf_op jit(solution)/shard_map/while/body/eval_jaxpr/reduce_sum | solution.py:22
  127.7 3.7 gather_fusion
  131.5 5.2 %multiply_reduce_fusion.2 = f32[64,200]{1,0:T(8,128)S(1)} fusion(f32[64,200,128]{2,1,0:T(8,128)} %gather_fusion, f32[64,128]{1,0:T(8,128)S(1)} %dynamic-slice_bitcast_fusion.2, pred[64]{0:T(512)(128)(4,1)S(1)} %compare_and_fusion.2), kind=kLoop, calls=%fused_computation.1.clone.1 | loop fusion | flops 4902400 | bytes 6637632 | tf_op jit(solution)/shard_map/while/body/eval_jaxpr/reduce_sum | solution.py:22
  136.7 3.7 gather_fusion
  140.5 5.2 %multiply_reduce_fusion.2 = f32[64,200]{1,0:T(8,128)S(1)} fusion(f32[64,200,128]{2,1,0:T(8,128)} %gather_fusion, f32[64,128]{1,0:T(8,128)S(1)} %dynamic-slice_bitcast_fusion.2, pred[64]{0:T(512)(128)(4,1)S(1)} %compare_and_fusion.2), kind=kLoop, calls=%fused_computation.1.clone.1 | loop fusion | flops 4902400 | bytes 6637632 | tf_op jit(solution)/shard_map/while/body/eval_jaxpr/reduce_sum | solution.py:22
  145.7 3.7 gather_fusion
  149.5 5.2 %multiply_reduce_fusion.2 = f32[64,200]{1,0:T(8,128)S(1)} fusion(f32[64,200,128]{2,1,0:T(8,128)} %gather_fusion, f32[64,128]{1,0:T(8,128)S(1)} %dynamic-slice_bitcast_fusion.2, pred[64]{0:T(512)(128)(4,1)S(1)} %compare_and_fusion.2), kind=kLoop, calls=%fused_computation.1.clone.1 | loop fusion | flops 4902400 | bytes 6637632 | tf_op jit(solution)/shard_map/while/body/eval_jaxpr/reduce_sum | solution.py:22
  156.1 47.5 %all-reduce.11.cloned.1.call-done = f32[200,1024]{1,0:T(8,128)} async-done(((f32[200,1024]{1,0:T(8,128)}), f32[200,1024]{1,0:T(8,128)}) %all-reduce.11.cloned.1.call-update) | async-done | bytes 819216 | tf_op jit(solution)/shard_map/psum | solution.py:42
  211.9 31.2 %all-reduce.17.cloned.1.call-done = (f32[200,200]{1,0:T(8,128)}, f32[200,200]{0,1:T(8,128)}) async-done(((f32[200,200]{1,0:T(8,128)}, f32[200,200]{0,1:T(8,128)}), (f32[200,200]{1,0:T(8,128)}, f32[200,200]{0,1:T(8,128)})) %all-reduce.17.cloned.1.call-update) | async-done | bytes 320016 | tf_op jit(solution)/shard_map/psum | solution.py:54
  245.2 11.7 %cholesky.182 = f32[128,128]{1,0:T(8,128)S(1)} custom-call(f32[128,128]{1,0:T(8,128)S(1)} %cholesky.292), custom_call_target="Cholesky" | custom-call | tf_op jit(solution)/shard_map/jit(cholesky)/cholesky | solution.py:55
  257.0 9.8 %custom-call.17 = f32[1,128,128]{1,2,0:T(8,128)S(1)} custom-call(f32[1,128,128]{2,1,0:T(8,128)S(1)} %get-tuple-element.95), custom_call_target="InvertDiagBlocksLowerTriangular" | custom-call | tf_op jit(solution)/shard_map/jit(cholesky)/cholesky | solution.py:55
  267.2 6.6 %cholesky.202 = f32[72,72]{1,0:T(8,128)S(1)} custom-call(f32[72,72]{1,0:T(8,128)S(1)} %convolution_subtract_fusion.8), custom_call_target="Cholesky" | custom-call | tf_op jit(solution)/shard_map/jit(cholesky)/cholesky | solution.py:55
  276.6 19.8 %custom-call.18 = f32[2,128,128]{1,2,0:T(8,128)S(1)} custom-call(f32[2,128,128]{2,1,0:T(8,128)S(1)} %pad_maximum_fusion.9), custom_call_target="InvertDiagBlocksLowerTriangular" | custom-call | tf_op jit(solution)/shard_map/jit(_cho_solve)/triangular_solve | solution.py:56
  306.6 32.8 %all-reduce.15.cloned.1.call-done = (f32[200,200]{1,0:T(8,128)}, f32[200,200]{0,1:T(8,128)}) async-done(((f32[200,200]{1,0:T(8,128)}, f32[200,200]{0,1:T(8,128)}), (f32[200,200]{1,0:T(8,128)}, f32[200,200]{0,1:T(8,128)})) %all-reduce.15.cloned.1.call-update) | async-done | bytes 320016 | tf_op jit(solution)/shard_map/psum | solution.py:54
  341.5 11.7 %cholesky.220 = f32[128,128]{1,0:T(8,128)S(1)} custom-call(f32[128,128]{1,0:T(8,128)S(1)} %cholesky.295), custom_call_target="Cholesky" | custom-call | tf_op jit(solution)/shard_map/jit(cholesky)/cholesky | solution.py:55
  353.3 9.8 %custom-call.19 = f32[1,128,128]{1,2,0:T(8,128)S(1)} custom-call(f32[1,128,128]{2,1,0:T(8,128)S(1)} %get-tuple-element.93), custom_call_target="InvertDiagBlocksLowerTriangular" | custom-call | tf_op jit(solution)/shard_map/jit(cholesky)/cholesky | solution.py:55
  363.5 6.6 %cholesky.240 = f32[72,72]{1,0:T(8,128)S(1)} custom-call(f32[72,72]{1,0:T(8,128)S(1)} %convolution_subtract_fusion.7), custom_call_target="Cholesky" | custom-call | tf_op jit(solution)/shard_map/jit(cholesky)/cholesky | solution.py:55
  372.9 19.9 %custom-call.20 = f32[2,128,128]{1,2,0:T(8,128)S(1)} custom-call(f32[2,128,128]{2,1,0:T(8,128)S(1)} %pad_maximum_fusion.10), custom_call_target="InvertDiagBlocksLowerTriangular" | custom-call | tf_op jit(solution)/shard_map/jit(_cho_solve)/triangular_solve | solution.py:56
  402.8 32.5 %all-reduce.13.cloned.1.call-done = (f32[200,200]{1,0:T(8,128)}, f32[200,200]{0,1:T(8,128)}) async-done(((f32[200,200]{1,0:T(8,128)}, f32[200,200]{0,1:T(8,128)}), (f32[200,200]{1,0:T(8,128)}, f32[200,200]{0,1:T(8,128)})) %all-reduce.13.cloned.1.call-update) | async-done | bytes 320016 | tf_op jit(solution)/shard_map/psum | solution.py:54
  437.3 11.7 %cholesky.258 = f32[128,128]{1,0:T(8,128)S(1)} custom-call(f32[128,128]{1,0:T(8,128)S(1)} %cholesky.298), custom_call_target="Cholesky" | custom-call | tf_op jit(solution)/shard_map/jit(cholesky)/cholesky | solution.py:55
  449.1 9.8 %custom-call.21 = f32[1,128,128]{1,2,0:T(8,128)S(1)} custom-call(f32[1,128,128]{2,1,0:T(8,128)S(1)} %get-tuple-element.91), custom_call_target="InvertDiagBlocksLowerTriangular" | custom-call | tf_op jit(solution)/shard_map/jit(cholesky)/cholesky | solution.py:55
  459.4 6.8 %cholesky.278 = f32[72,72]{1,0:T(8,128)S(1)} custom-call(f32[72,72]{1,0:T(8,128)S(1)} %convolution_subtract_fusion.6), custom_call_target="Cholesky" | custom-call | tf_op jit(solution)/shard_map/jit(cholesky)/cholesky | solution.py:55
  469.0 19.7 %custom-call.22 = f32[2,128,128]{1,2,0:T(8,128)S(1)} custom-call(f32[2,128,128]{2,1,0:T(8,128)S(1)} %pad_maximum_fusion.11), custom_call_target="InvertDiagBlocksLowerTriangular" | custom-call | tf_op jit(solution)/shard_map/jit(_cho_solve)/triangular_solve | solution.py:56
  (195 shorter events, 56.3 us)
Async XLA Ops:
  7.2 196.4 %all-reduce.11.cloned.1.call-start = ((), (), s32[]{:S(2)}) async-start(), calls=%async_computation | async-start | bytes 1638400 | tf_op jit(solution)/shard_map/psum | solution.py:42
  10.8 145.2 %copy-start.1 = (bf16[200,512]{1,0:T(8,128)(2,1)S(1)}, bf16[200,512]{1,0:T(8,128)(2,1)}, u32[]{:S(2)}) copy-start(bf16[200,512]{1,0:T(8,128)(2,1)} %param.11) | copy-start | bytes 614404
  10.8 145.3 %copy-start.2 = (f32[1024]{0:T(1024)S(1)}, f32[1024]{0:T(1024)}, u32[]{:S(2)}) copy-start(f32[1024]{0:T(1024)} %param.15) | copy-start | bytes 12292
  154.7 53.1 %copy-start.3 = (f32[1024]{0:T(1024)S(1)}, f32[1024]{0:T(1024)}, u32[]{:S(2)}) copy-start(f32[1024]{0:T(1024)} %param.14) | copy-start | bytes 12292
  155.9 87.2 %all-reduce.17.cloned.1.call-start = ((), (), s32[]{:S(2)}) async-start(), calls=%async_computation.3 | async-start | bytes 819200 | tf_op jit(solution)/shard_map/psum | solution.py:54
  207.8 92.5 %copy-start = (f32[200,1024]{1,0:T(8,128)S(1)}, f32[200,1024]{1,0:T(8,128)}, u32[]{:S(2)}) copy-start(f32[200,1024]{1,0:T(8,128)} %all-reduce.11.cloned.1.call-done) | copy-start | bytes 2457604
  211.3 128.2 %all-reduce.15.cloned.1.call-start = ((), (), s32[]{:S(2)}) async-start(), calls=%async_computation.2 | async-start | bytes 819200 | tf_op jit(solution)/shard_map/psum | solution.py:54
  306.4 128.9 %all-reduce.13.cloned.1.call-start = ((), (), s32[]{:S(2)}) async-start(), calls=%async_computation.1 | async-start | bytes 819200 | tf_op jit(solution)/shard_map/psum | solution.py:54
Sparse Core Ops, SparseCore 0:
  156.1 47.4 all-reduce.10
  211.4 31.6 all-reduce.16
  306.5 32.9 all-reduce.14
  402.3 32.9 all-reduce.12
where the time goes:
time: 508 us; the launch traced here: 503 us
  other arithmetic  242 us (48%)
  waiting for transfers between devices  144 us (28%)
  local copies, waits for them, and re-layouts  61.6 us (12%)
  matrix products  33.9 us (7%)
  between operations  18.7 us (4%)
    psum x3, waiting for transfers between devices, per_device(): gram_matrix, cross_term = lax.psum((gram_matrix, cross_term), 'obs')  96.6 us
    another operation x21, other arithmetic, per_device(): factor = jnp.linalg.cholesky(gram_matrix + inflation * identity)  88.6 us
    reduce_sum x16, other arithmetic, one_group(): return jnp.sum(picked * group_weight[None], axis=2)  83 us
    another operation x14, other arithmetic, per_device(): member_weight = jax.scipy.linalg.cho_solve((factor, True), cross_term)  59.8 us
    gather x16, local copies, waits for them, and re-layouts, one_group(): picked = jnp.take(blocks, group_index, axis=1)  59.3 us
    psum x1, waiting for transfers between devices, per_device(): predicted = lax.psum(partial_terms, 'cell')  47.5 us
    another operation x18, matrix products, per_device(): member_weight = jax.scipy.linalg.cho_solve((factor, True), cross_term)  11.1 us
  transfers between devices with their start and end apart: 4, of which 4 were waited for; matrix products, arithmetic and copies ran while one was open for 0% of the time, Pallas kernels for 0%

commit v1 on v0

--- a/solution.py
+++ b/solution.py
@@ -1,3 +1,4 @@
+import functools
 import jax
 import jax.numpy as jnp
 from jax import lax
@@ -5,6 +6,17 @@
 
 BLK = 128
 ITERS = 3
+
+
+def supply_all_core(v0, along_axis):
+    wide_n = lax.axis_size(along_axis)
+    y = v0
+    for k in [s for s in (1, 2, 4, 8, 16) if s < wide_n]:
+        y = y + lax.ppermute(y, along_axis, [(it, it ^ k) for it in range(wide_n)])
+    return y
+
+
+obtain_kinds = functools.partial(supply_all_core, along_axis="cell")
 
 
 def local_partial(param_field, local_index, weights):
@@ -39,7 +51,7 @@
     root_scale = jnp.sqrt(jnp.float32(members - 1.0))
     identity = jnp.eye(members, dtype=jnp.float32)
     partial_terms = local_partial(param_field, clipped, weights)
-    predicted = lax.psum(partial_terms, "cell")
+    predicted = obtain_kinds(partial_terms)
     for step_index in range(ITERS):
         noise = jnp.sqrt(jnp.float32(3.0)) * (
             (2.0 * pert_seed[step_index].astype(jnp.float32) + 1.0) / 1048576.0 - 1.0

time: 508 us -> 518 us (1.020)
  waiting for transfers between devices: 144 us -> 152 us
  starting transfers between devices: 0.9 us -> 6.84 us
    ppermute x0 -> x2, waiting for transfers between devices: none -> 53.3 us  [supply_all_core(): y = y + lax.ppermute(y, along_axis, [(it, it ^ k) for it in range(wide_n)])]
    psum x1 -> x0, waiting for transfers between devices: 47.5 us -> none  [per_device(): predicted = lax.psum(partial_terms, 'cell')]
    ppermute x0 -> x2, starting transfers between devices: none -> 5.98 us  [supply_all_core(): y = y + lax.ppermute(y, along_axis, [(it, it ^ k) for it in range(wide_n)])]
  transfers between devices with their start and end apart: 4 -> 5, of which waited for: 4 -> 5; matrix products, arithmetic and copies ran while one was open for 0% -> 0% of each run, Pallas kernels for 0% -> 0%
where the time goes in v1:
time: 518 us; the launch traced here: 512 us
  other arithmetic  241 us (47%)
  waiting for transfers between devices  152 us (29%)
  local copies, waits for them, and re-layouts  60.7 us (12%)
  matrix products  32 us (6%)
  between operations  18.7 us (4%)
  starting transfers between devices  6.84 us (1%)
    psum x3, waiting for transfers between devices, per_device(): gram_matrix, cross_term = lax.psum((gram_matrix, cross_term), 'obs')  98.7 us
    another operation x21, other arithmetic, per_device(): factor = jnp.linalg.cholesky(gram_matrix + inflation * identity)  88.6 us
    reduce_sum x16, other arithmetic, one_group(): return jnp.sum(picked * group_weight[None], axis=2)  83 us
    another operation x14, other arithmetic, per_device(): member_weight = jax.scipy.linalg.cho_solve((factor, True), cross_term)  59.8 us
    gather x16, local copies, waits for them, and re-layouts, one_group(): picked = jnp.take(blocks, group_index, axis=1)  59.3 us
    ppermute x2, waiting for transfers between devices, supply_all_core(): y = y + lax.ppermute(y, along_axis, [(it, it ^ k) for it in range(wide_n)])  53.3 us
    another operation x18, matrix products, per_device(): member_weight = jax.scipy.linalg.cho_solve((factor, True), cross_term)  11.1 us
  transfers between devices with their start and end apart: 5, of which 5 were waited for; matrix products, arithmetic and copies ran while one was open for 0% of the time, Pallas kernels for 0%

profile of v1, /device:TPU:0, one launch (start us, length us, event | category | flops | bytes accessed | tf_op | source)
XLA Modules:
  0.0 512.4 jit_solution(2806110637296299627)
XLA Ops:
  10.8 143.9 %while.14 = (s32[]{:T(128)}, f32[16,200,64]{1,2,0:T(8,128)S(1)}, s32[16,64]{1,0:T(8,128)S(1)}, f32[200,4,128]{2,0,1:T(8,128)S(1)}, f32[16,64,128]{2,1,0:T(8,128)S(1)}, /*index=5*/s32[]{:T(128)}) while((s32[]{:T(128)}, f32[16,200,64]{1,2,0:T(8,128)S(1)}, s32[16,64]{1,0:T(8,128)S(1)}, f32[200,4,128]{2,0,1:T(8,128)S(1)}, ...), condition=%wide.region_2.3_spmd, body=%wide.region_0.2_spmd.sunk | while | flops 4904002 | bytes 19946964 | solution.py:36
  10.9 3.7 gather_fusion
  14.6 5.2 %multiply_reduce_fusion.2 = f32[64,200]{1,0:T(8,128)S(1)} fusion(f32[64,200,128]{2,1,0:T(8,128)} %gather_fusion, f32[64,128]{1,0:T(8,128)S(1)} %dynamic-slice_bitcast_fusion.2, pred[64]{0:T(512)(128)(4,1)S(1)} %compare_and_fusion.2), kind=kLoop, calls=%fused_computation.1.clone.1 | loop fusion | flops 4902400 | bytes 6637632 | tf_op jit(solution)/shard_map/while/body/eval_jaxpr/reduce_sum | solution.py:34
  19.8 3.7 gather_fusion
  23.6 5.2 %multiply_reduce_fusion.2 = f32[64,200]{1,0:T(8,128)S(1)} fusion(f32[64,200,128]{2,1,0:T(8,128)} %gather_fusion, f32[64,128]{1,0:T(8,128)S(1)} %dynamic-slice_bitcast_fusion.2, pred[64]{0:T(512)(128)(4,1)S(1)} %compare_and_fusion.2), kind=kLoop, calls=%fused_computation.1.clone.1 | loop fusion | flops 4902400 | bytes 6637632 | tf_op jit(solution)/shard_map/while/body/eval_jaxpr/reduce_sum | solution.py:34
  28.8 3.7 gather_fusion
  32.6 5.2 %multiply_reduce_fusion.2 = f32[64,200]{1,0:T(8,128)S(1)} fusion(f32[64,200,128]{2,1,0:T(8,128)} %gather_fusion, f32[64,128]{1,0:T(8,128)S(1)} %dynamic-slice_bitcast_fusion.2, pred[64]{0:T(512)(128)(4,1)S(1)} %compare_and_fusion.2), kind=kLoop, calls=%fused_computation.1.clone.1 | loop fusion | flops 4902400 | bytes 6637632 | tf_op jit(solution)/shard_map/while/body/eval_jaxpr/reduce_sum | solution.py:34
  37.8 3.7 gather_fusion
  41.6 5.2 %multiply_reduce_fusion.2 = f32[64,200]{1,0:T(8,128)S(1)} fusion(f32[64,200,128]{2,1,0:T(8,128)} %gather_fusion, f32[64,128]{1,0:T(8,128)S(1)} %dynamic-slice_bitcast_fusion.2, pred[64]{0:T(512)(128)(4,1)S(1)} %compare_and_fusion.2), kind=kLoop, calls=%fused_computation.1.clone.1 | loop fusion | flops 4902400 | bytes 6637632 | tf_op jit(solution)/shard_map/while/body/eval_jaxpr/reduce_sum | solution.py:34
  46.8 3.7 gather_fusion
  50.6 5.2 %multiply_reduce_fusion.2 = f32[64,200]{1,0:T(8,128)S(1)} fusion(f32[64,200,128]{2,1,0:T(8,128)} %gather_fusion, f32[64,128]{1,0:T(8,128)S(1)} %dynamic-slice_bitcast_fusion.2, pred[64]{0:T(512)(128)(4,1)S(1)} %compare_and_fusion.2), kind=kLoop, calls=%fused_computation.1.clone.1 | loop fusion | flops 4902400 | bytes 6637632 | tf_op jit(solution)/shard_map/while/body/eval_jaxpr/reduce_sum | solution.py:34
  55.8 3.7 gather_fusion
  59.5 5.2 %multiply_reduce_fusion.2 = f32[64,200]{1,0:T(8,128)S(1)} fusion(f32[64,200,128]{2,1,0:T(8,128)} %gather_fusion, f32[64,128]{1,0:T(8,128)S(1)} %dynamic-slice_bitcast_fusion.2, pred[64]{0:T(512)(128)(4,1)S(1)} %compare_and_fusion.2), kind=kLoop, calls=%fused_computation.1.clone.1 | loop fusion | flops 4902400 | bytes 6637632 | tf_op jit(solution)/shard_map/while/body/eval_jaxpr/reduce_sum | solution.py:34
  64.8 3.7 gather_fusion
  68.5 5.2 %multiply_reduce_fusion.2 = f32[64,200]{1,0:T(8,128)S(1)} fusion(f32[64,200,128]{2,1,0:T(8,128)} %gather_fusion, f32[64,128]{1,0:T(8,128)S(1)} %dynamic-slice_bitcast_fusion.2, pred[64]{0:T(512)(128)(4,1)S(1)} %compare_and_fusion.2), kind=kLoop, calls=%fused_computation.1.clone.1 | loop fusion | flops 4902400 | bytes 6637632 | tf_op jit(solution)/shard_map/while/body/eval_jaxpr/reduce_sum | solution.py:34
  73.8 3.7 gather_fusion
  77.5 5.2 %multiply_reduce_fusion.2 = f32[64,200]{1,0:T(8,128)S(1)} fusion(f32[64,200,128]{2,1,0:T(8,128)} %gather_fusion, f32[64,128]{1,0:T(8,128)S(1)} %dynamic-slice_bitcast_fusion.2, pred[64]{0:T(512)(128)(4,1)S(1)} %compare_and_fusion.2), kind=kLoop, calls=%fused_computation.1.clone.1 | loop fusion | flops 4902400 | bytes 6637632 | tf_op jit(solution)/shard_map/while/body/eval_jaxpr/reduce_sum | solution.py:34
  82.8 3.7 gather_fusion
  86.5 5.2 %multiply_reduce_fusion.2 = f32[64,200]{1,0:T(8,128)S(1)} fusion(f32[64,200,128]{2,1,0:T(8,128)} %gather_fusion, f32[64,128]{1,0:T(8,128)S(1)} %dynamic-slice_bitcast_fusion.2, pred[64]{0:T(512)(128)(4,1)S(1)} %compare_and_fusion.2), kind=kLoop, calls=%fused_computation.1.clone.1 | loop fusion | flops 4902400 | bytes 6637632 | tf_op jit(solution)/shard_map/while/body/eval_jaxpr/reduce_sum | solution.py:34
  91.8 3.7 gather_fusion
  95.5 5.2 %multiply_reduce_fusion.2 = f32[64,200]{1,0:T(8,128)S(1)} fusion(f32[64,200,128]{2,1,0:T(8,128)} %gather_fusion, f32[64,128]{1,0:T(8,128)S(1)} %dynamic-slice_bitcast_fusion.2, pred[64]{0:T(512)(128)(4,1)S(1)} %compare_and_fusion.2), kind=kLoop, calls=%fused_computation.1.clone.1 | loop fusion | flops 4902400 | bytes 6637632 | tf_op jit(solution)/shard_map/while/body/eval_jaxpr/reduce_sum | solution.py:34
  100.8 3.7 gather_fusion
  104.5 5.2 %multiply_reduce_fusion.2 = f32[64,200]{1,0:T(8,128)S(1)} fusion(f32[64,200,128]{2,1,0:T(8,128)} %gather_fusion, f32[64,128]{1,0:T(8,128)S(1)} %dynamic-slice_bitcast_fusion.2, pred[64]{0:T(512)(128)(4,1)S(1)} %compare_and_fusion.2), kind=kLoop, calls=%fused_computation.1.clone.1 | loop fusion | flops 4902400 | bytes 6637632 | tf_op jit(solution)/shard_map/while/body/eval_jaxpr/reduce_sum | solution.py:34
  109.8 3.7 gather_fusion
  113.5 5.2 %multiply_reduce_fusion.2 = f32[64,200]{1,0:T(8,128)S(1)} fusion(f32[64,200,128]{2,1,0:T(8,128)} %gather_fusion, f32[64,128]{1,0:T(8,128)S(1)} %dynamic-slice_bitcast_fusion.2, pred[64]{0:T(512)(128)(4,1)S(1)} %compare_and_fusion.2), kind=kLoop, calls=%fused_computation.1.clone.1 | loop fusion | flops 4902400 | bytes 6637632 | tf_op jit(solution)/shard_map/while/body/eval_jaxpr/reduce_sum | solution.py:34
  122.5 5.2 %multiply_reduce_fusion.2 = f32[64,200]{1,0:T(8,128)S(1)} fusion(f32[64,200,128]{2,1,0:T(8,128)} %gather_fusion, f32[64,128]{1,0:T(8,128)S(1)} %dynamic-slice_bitcast_fusion.2, pred[64]{0:T(512)(128)(4,1)S(1)} %compare_and_fusion.2), kind=kLoop, calls=%fused_computation.1.clone.1 | loop fusion | flops 4902400 | bytes 6637632 | tf_op jit(solution)/shard_map/while/body/eval_jaxpr/reduce_sum | solution.py:34
  131.5 5.2 %multiply_reduce_fusion.2 = f32[64,200]{1,0:T(8,128)S(1)} fusion(f32[64,200,128]{2,1,0:T(8,128)} %gather_fusion, f32[64,128]{1,0:T(8,128)S(1)} %dynamic-slice_bitcast_fusion.2, pred[64]{0:T(512)(128)(4,1)S(1)} %compare_and_fusion.2), kind=kLoop, calls=%fused_computation.1.clone.1 | loop fusion | flops 4902400 | bytes 6637632 | tf_op jit(solution)/shard_map/while/body/eval_jaxpr/reduce_sum | solution.py:34
  136.7 3.7 gather_fusion
  140.5 5.2 %multiply_reduce_fusion.2 = f32[64,200]{1,0:T(8,128)S(1)} fusion(f32[64,200,128]{2,1,0:T(8,128)} %gather_fusion, f32[64,128]{1,0:T(8,128)S(1)} %dynamic-slice_bitcast_fusion.2, pred[64]{0:T(512)(128)(4,1)S(1)} %compare_and_fusion.2), kind=kLoop, calls=%fused_computation.1.clone.1 | loop fusion | flops 4902400 | bytes 6637632 | tf_op jit(solution)/shard_map/while/body/eval_jaxpr/reduce_sum | solution.py:34
  145.7 3.7 gather_fusion
  149.5 5.2 %multiply_reduce_fusion.2 = f32[64,200]{1,0:T(8,128)S(1)} fusion(f32[64,200,128]{2,1,0:T(8,128)} %gather_fusion, f32[64,128]{1,0:T(8,128)S(1)} %dynamic-slice_bitcast_fusion.2, pred[64]{0:T(512)(128)(4,1)S(1)} %compare_and_fusion.2), kind=kLoop, calls=%fused_computation.1.clone.1 | loop fusion | flops 4902400 | bytes 6637632 | tf_op jit(solution)/shard_map/while/body/eval_jaxpr/reduce_sum | solution.py:34
  158.2 18.2 %collective-permute-done = f32[200,1024]{1,0:T(8,128)S(1)} collective-permute-done((f32[200,1024]{1,0:T(8,128)S(1)}, f32[200,1024]{1,0:T(8,128)S(1)}, u32[]{:S(2)}, u32[]{:S(2)}) %collective-permute-start) | collective-permute-done | bytes 819232 | tf_op jit(solution)/shard_map/ppermute | solution.py:15
  179.4 35.0 %collective-permute-done.1 = f32[200,1024]{1,0:T(8,128)S(1)} collective-permute-done((f32[200,1024]{1,0:T(8,128)S(1)}, f32[200,1024]{1,0:T(8,128)S(1)}, u32[]{:S(2)}, u32[]{:S(2)}) %collective-permute-start.1) | collective-permute-done | bytes 819232 | tf_op jit(solution)/shard_map/ppermute | solution.py:15
  219.7 33.3 %all-reduce.14.cloned.1.call-done = (f32[200,200]{1,0:T(8,128)}, f32[200,200]{0,1:T(8,128)}) async-done(((f32[200,200]{1,0:T(8,128)}, f32[200,200]{0,1:T(8,128)}), (f32[200,200]{1,0:T(8,128)}, f32[200,200]{0,1:T(8,128)})) %all-reduce.14.cloned.1.call-update) | async-done | bytes 320016 | tf_op jit(solution)/shard_map/psum | solution.py:66
  255.1 11.7 %cholesky.182 = f32[128,128]{1,0:T(8,128)S(1)} custom-call(f32[128,128]{1,0:T(8,128)S(1)} %cholesky.292), custom_call_target="Cholesky" | custom-call | tf_op jit(solution)/shard_map/jit(cholesky)/cholesky | solution.py:67
  266.8 9.8 %custom-call.17 = f32[1,128,128]{1,2,0:T(8,128)S(1)} custom-call(f32[1,128,128]{2,1,0:T(8,128)S(1)} %get-tuple-element.97), custom_call_target="InvertDiagBlocksLowerTriangular" | custom-call | tf_op jit(solution)/shard_map/jit(cholesky)/cholesky | solution.py:67
  277.1 6.6 %cholesky.202 = f32[72,72]{1,0:T(8,128)S(1)} custom-call(f32[72,72]{1,0:T(8,128)S(1)} %convolution_subtract_fusion.8), custom_call_target="Cholesky" | custom-call | tf_op jit(solution)/shard_map/jit(cholesky)/cholesky | solution.py:67
  286.5 19.8 %custom-call.18 = f32[2,128,128]{1,2,0:T(8,128)S(1)} custom-call(f32[2,128,128]{2,1,0:T(8,128)S(1)} %pad_maximum_fusion.9), custom_call_target="InvertDiagBlocksLowerTriangular" | custom-call | tf_op jit(solution)/shard_map/jit(_cho_solve)/triangular_solve | solution.py:68
  316.5 32.8 %all-reduce.12.cloned.1.call-done = (f32[200,200]{1,0:T(8,128)}, f32[200,200]{0,1:T(8,128)}) async-done(((f32[200,200]{1,0:T(8,128)}, f32[200,200]{0,1:T(8,128)}), (f32[200,200]{1,0:T(8,128)}, f32[200,200]{0,1:T(8,128)})) %all-reduce.12.cloned.1.call-update) | async-done | bytes 320016 | tf_op jit(solution)/shard_map/psum | solution.py:66
  351.4 11.7 %cholesky.220 = f32[128,128]{1,0:T(8,128)S(1)} custom-call(f32[128,128]{1,0:T(8,128)S(1)} %cholesky.295), custom_call_target="Cholesky" | custom-call | tf_op jit(solution)/shard_map/jit(cholesky)/cholesky | solution.py:67
  363.2 9.8 %custom-call.19 = f32[1,128,128]{1,2,0:T(8,128)S(1)} custom-call(f32[1,128,128]{2,1,0:T(8,128)S(1)} %get-tuple-element.95), custom_call_target="InvertDiagBlocksLowerTriangular" | custom-call | tf_op jit(solution)/shard_map/jit(cholesky)/cholesky | solution.py:67
  373.4 6.6 %cholesky.240 = f32[72,72]{1,0:T(8,128)S(1)} custom-call(f32[72,72]{1,0:T(8,128)S(1)} %convolution_subtract_fusion.7), custom_call_target="Cholesky" | custom-call | tf_op jit(solution)/shard_map/jit(cholesky)/cholesky | solution.py:67
  382.8 19.9 %custom-call.20 = f32[2,128,128]{1,2,0:T(8,128)S(1)} custom-call(f32[2,128,128]{2,1,0:T(8,128)S(1)} %pad_maximum_fusion.10), custom_call_target="InvertDiagBlocksLowerTriangular" | custom-call | tf_op jit(solution)/shard_map/jit(_cho_solve)/triangular_solve | solution.py:68
  412.6 32.5 %all-reduce.10.cloned.1.call-done = (f32[200,200]{1,0:T(8,128)}, f32[200,200]{0,1:T(8,128)}) async-done(((f32[200,200]{1,0:T(8,128)}, f32[200,200]{0,1:T(8,128)}), (f32[200,200]{1,0:T(8,128)}, f32[200,200]{0,1:T(8,128)})) %all-reduce.10.cloned.1.call-update) | async-done | bytes 320016 | tf_op jit(solution)/shard_map/psum | solution.py:66
  447.2 11.7 %cholesky.258 = f32[128,128]{1,0:T(8,128)S(1)} custom-call(f32[128,128]{1,0:T(8,128)S(1)} %cholesky.298), custom_call_target="Cholesky" | custom-call | tf_op jit(solution)/shard_map/jit(cholesky)/cholesky | solution.py:67
  459.0 9.8 %custom-call.21 = f32[1,128,128]{1,2,0:T(8,128)S(1)} custom-call(f32[1,128,128]{2,1,0:T(8,128)S(1)} %get-tuple-element.93), custom_call_target="InvertDiagBlocksLowerTriangular" | custom-call | tf_op jit(solution)/shard_map/jit(cholesky)/cholesky | solution.py:67
  469.3 6.8 %cholesky.278 = f32[72,72]{1,0:T(8,128)S(1)} custom-call(f32[72,72]{1,0:T(8,128)S(1)} %convolution_subtract_fusion.6), custom_call_target="Cholesky" | custom-call | tf_op jit(solution)/shard_map/jit(cholesky)/cholesky | solution.py:67
  478.9 19.7 %custom-call.22 = f32[2,128,128]{1,2,0:T(8,128)S(1)} custom-call(f32[2,128,128]{2,1,0:T(8,128)S(1)} %pad_maximum_fusion.11), custom_call_target="InvertDiagBlocksLowerTriangular" | custom-call | tf_op jit(solution)/shard_map/jit(_cho_solve)/triangular_solve | solution.py:68
  (195 shorter events, 62.1 us)
Async XLA Ops:
  7.2 245.9 %all-reduce.14.cloned.1.call-start = ((), (), s32[]{:S(2)}) async-start(), calls=%async_computation.2 | async-start | bytes 819200 | tf_op jit(solution)/shard_map/psum | solution.py:66
  10.8 168.6 %copy-start = (bf16[200,512]{1,0:T(8,128)(2,1)S(1)}, bf16[200,512]{1,0:T(8,128)(2,1)}, u32[]{:S(2)}) copy-start(bf16[200,512]{1,0:T(8,128)(2,1)} %param.11) | copy-start | bytes 614404
  10.8 168.6 %copy-start.1 = (f32[1024]{0:T(1024)S(1)}, f32[1024]{0:T(1024)}, u32[]{:S(2)}) copy-start(f32[1024]{0:T(1024)} %param.15) | copy-start | bytes 12292
  154.7 61.5 %copy-start.2 = (f32[1024]{0:T(1024)S(1)}, f32[1024]{0:T(1024)}, u32[]{:S(2)}) copy-start(f32[1024]{0:T(1024)} %param.14) | copy-start | bytes 12292
  155.0 21.4 %collective-permute-start = (f32[200,1024]{1,0:T(8,128)S(1)}, f32[200,1024]{1,0:T(8,128)S(1)}, u32[]{:S(2)}, u32[]{:S(2)}) collective-permute-start(f32[200,1024]{1,0:T(8,128)S(1)} %copy.33), channel_id=1, source_target_pairs={{0,4},{4,0},{8,12},{12,8},{1,5},{5,1},{9,13},{13,9},{2,6},{6,2},{1... | collective-permute-start | bytes 2457608 | tf_op jit(solution)/shard_map/ppermute | solution.py:15
  176.5 37.9 %collective-permute-start.1 = (f32[200,1024]{1,0:T(8,128)S(1)}, f32[200,1024]{1,0:T(8,128)S(1)}, u32[]{:S(2)}, u32[]{:S(2)}) collective-permute-start(f32[200,1024]{1,0:T(8,128)S(1)} %add.126), channel_id=1, source_target_pairs={{0,8},{4,12},{8,0},{12,4},{1,9},{5,13},{9,1},{13,5},{2,10},{6,14},... | collective-permute-start | bytes 2457608 | tf_op jit(solution)/shard_map/ppermute | solution.py:15
  219.1 130.2 %all-reduce.12.cloned.1.call-start = ((), (), s32[]{:S(2)}) async-start(), calls=%async_computation.1 | async-start | bytes 819200 | tf_op jit(solution)/shard_map/psum | solution.py:66
  316.2 128.9 %all-reduce.10.cloned.1.call-start = ((), (), s32[]{:S(2)}) async-start(), calls=%async_computation | async-start | bytes 819200 | tf_op jit(solution)/shard_map/psum | solution.py:66
Sparse Core Ops, SparseCore 0:
  219.3 33.7 all-reduce.13
  316.4 32.9 all-reduce.11
  412.2 32.9 all-reduce.9
